TPU v7x, 32 devices: a whole 2x2x4 slice. The times are simulated.
32 devices in a mesh: clip: 4 (over z), tm: 8 (over y, x, core).
Axes of the slice: x: 2, y: 2, z: 4, core: 2. Of those that a mesh axis runs over, the one named last changes fastest.
Arguments:
- tokens: bfloat16 [4, 8, 256, 2048], P('clip', 'tm'), may hold values from -16 to 16
- spatial_queries: bfloat16 [4, 8, 256, 1024], P('clip', 'tm'), may hold values from -4.5 to 4.5
- spatial_keys: bfloat16 [4, 8, 256, 1024], P('clip', 'tm'), may hold values from -4.5 to 4.5
- spatial_values: bfloat16 [4, 8, 256, 1024], P('clip', 'tm'), may hold values from -6 to 6
- spatial_proj: bfloat16 [1024, 2048], P('tm'), may hold values from -0.1875 to 0.1875
- temporal_qkv: bfloat16 [2048, 3072], P('tm'), may hold values from -0.13258252 to 0.13258252
- temporal_proj: bfloat16 [1024, 2048], P('tm'), may hold values from -0.1875 to 0.1875
- frame_mask: int32 [4, 8, 8], P('clip'), may hold values from 0 to 1, as said below
- expert_ids: int32 [4, 8, 256, 2], P('clip', 'tm'), may hold values from 0 to 31, all different within a row; in each aligned block of 256 rows (0 to 255, 256 to 511, ..., all dimensions but the last counted through in order) at most 32 rows name the same one
- gate_values: float32 [4, 8, 256, 2], P('clip', 'tm'), may hold values from 0.2 to 1
- expert_gate: bfloat16 [32, 2048, 1408], P(('clip', 'tm')), may hold values from -0.125 to 0.125
- expert_up: bfloat16 [32, 2048, 1408], P(('clip', 'tm')), may hold values from -0.125 to 0.125
- expert_down: bfloat16 [32, 1408, 2048], P(('clip', 'tm')), may hold values from -0.15625 to 0.15625
Outputs:
- layer_out: bfloat16 [4, 8, 256, 2048], P('clip', 'tm')
Inputs may be any that keep to these rules, and one draw needn't show every extreme that they name: `expert_ids`: each token names 2 different experts. Among the 256 tokens of one clip and frame, no expert is named by more than 32 tokens, and in some frames one expert is named by exactly 32. frame_mask[c, i, j] is 1 where j = i and 0 where j > i.
All inputs are finite; a program needn't handle non-finite values.
Results may differ from a plain program's by a relative error of at most 0.013.
Values may be sent and summed in bfloat16 or wider, within the bound.
A program may use at most 128 MiB of HBM per device.

v0:
```python
import math

import jax
import jax.numpy as jnp
from jax import lax
from jax.sharding import PartitionSpec as P

HEADS = 8
HD = 128
TOP = 2


EPS = 1e-06
MASKED = -1e30


def rms_normed(values):
    wide = values.astype(jnp.float32)
    inverse = lax.rsqrt(jnp.mean(wide * wide, axis=-1, keepdims=True) + EPS)
    return (wide * inverse).astype(jnp.bfloat16)


def normalize_rows(scores):
    row_max = jnp.max(scores, axis=-1, keepdims=True)
    exp_terms = jnp.exp(scores - row_max)
    return (exp_terms / jnp.sum(exp_terms, axis=-1, keepdims=True)).astype(jnp.bfloat16)


def add_columns(left_side, piece):
    return jnp.dot(left_side, piece, preferred_element_type=jnp.float32)


def spatial_mix(queries, keys, values):
    positions = queries.shape[0]
    score_scale = 1.0 / math.sqrt(HD)
    query_heads = queries.reshape(positions, HEADS, HD)
    key_heads = keys.reshape(positions, HEADS, HD)
    value_heads = values.reshape(positions, HEADS, HD)
    scores = (
        jnp.einsum("qhd,khd->hqk", query_heads, key_heads, preferred_element_type=jnp.float32)
        * score_scale
    )
    weights = normalize_rows(scores)
    mixed = jnp.einsum("hqk,khd->qhd", weights, value_heads, preferred_element_type=jnp.float32)
    return mixed.astype(jnp.bfloat16).reshape(positions, HEADS * HD)


def temporal_mix(queries, keys, values, allowed):
    frames, positions = (queries.shape[0], queries.shape[1])
    score_scale = 1.0 / math.sqrt(HD)
    query_heads = queries.reshape(frames, positions, HEADS, HD)
    key_heads = keys.reshape(frames, positions, HEADS, HD)
    value_heads = values.reshape(frames, positions, HEADS, HD)
    scores = (
        jnp.einsum("iphd,jphd->phij", query_heads, key_heads, preferred_element_type=jnp.float32)
        * score_scale
    )
    weights = normalize_rows(jnp.where(allowed[None, None, :, :], scores, MASKED))
    mixed = jnp.einsum("phij,jphd->iphd", weights, value_heads, preferred_element_type=jnp.float32)
    return mixed.astype(jnp.bfloat16).reshape(frames, positions, HEADS * HD)


def temporal_inputs(normed, qkv_rows):
    zero_start = jnp.zeros((normed.shape[0], qkv_rows.shape[1]), jnp.float32)

    def fold_rows(total, piece, start):
        return add_columns(normed, piece)

    return fold_rows(
        zero_start, lax.all_gather(qkv_rows, "tm", axis=0, tiled=True), jnp.int32(0)
    ).astype(jnp.bfloat16)


def temporal_output(mixed, proj_rows):
    zero_start = jnp.zeros((mixed.shape[0], proj_rows.shape[1]), jnp.float32)

    def fold_rows(total, piece, start):
        return add_columns(mixed, piece)

    return fold_rows(
        zero_start, lax.all_gather(proj_rows, "tm", axis=0, tiled=True), jnp.int32(0)
    ).astype(jnp.bfloat16)


def shards(
    tokens,
    spatial_queries,
    spatial_keys,
    spatial_values,
    spatial_proj,
    temporal_qkv,
    temporal_proj,
    frame_mask,
    expert_ids,
    gate_values,
    expert_gate,
    expert_up,
    expert_down,
):
    model_width = tokens.shape[3]
    positions = tokens.shape[2]
    tm_count = lax.axis_size("tm")
    clip_count = lax.axis_size("clip")
    experts = clip_count * tm_count
    per_block = positions // tm_count
    resident = tokens.reshape(positions, model_width)
    attended_space = spatial_mix(
        spatial_queries.reshape(positions, -1),
        spatial_keys.reshape(positions, -1),
        spatial_values.reshape(positions, -1),
    )
    spatial_update = add_columns(
        attended_space, lax.all_gather(spatial_proj, "tm", axis=0, tiled=True)
    )
    first = (resident.astype(jnp.float32) + spatial_update).astype(jnp.bfloat16)
    normed = rms_normed(first)
    allowed = frame_mask[0] == 1
    by_position = lax.all_to_all(
        normed.reshape(tm_count, per_block, model_width),
        "tm",
        split_axis=0,
        concat_axis=0,
        tiled=True,
    )
    frames = by_position.shape[0]
    projected = temporal_inputs(by_position.reshape(frames * per_block, model_width), temporal_qkv)
    head_width = projected.shape[1] // 3
    triple = projected.reshape(frames, per_block, 3 * head_width)
    attended_time = temporal_mix(
        triple[:, :, :head_width],
        triple[:, :, head_width : 2 * head_width],
        triple[:, :, 2 * head_width :],
        allowed,
    )
    update_rows = temporal_output(
        attended_time.reshape(frames * per_block, head_width), temporal_proj
    )
    returned = lax.all_to_all(
        update_rows.reshape(frames, per_block, model_width),
        "tm",
        split_axis=0,
        concat_axis=0,
        tiled=True,
    )
    temporal_update = returned.reshape(positions, model_width)
    second = (first.astype(jnp.float32) + temporal_update.astype(jnp.float32)).astype(jnp.bfloat16)
    routed = rms_normed(second)
    capacity = 2 * TOP * positions // experts
    slot_count = experts * capacity
    pair_ids = expert_ids.reshape(positions * TOP)
    chosen = (pair_ids[:, None] == jnp.arange(experts, dtype=jnp.int32)[None, :]).astype(jnp.int32)
    earlier = jnp.cumsum(chosen, axis=0) - chosen
    pair_rank = jnp.sum(earlier * chosen, axis=1)
    pair_slot = pair_ids * capacity + pair_rank
    slot_index = jnp.arange(slot_count, dtype=jnp.int32)
    pair_onehot = (pair_slot[:, None] == slot_index[None, :]).astype(jnp.bfloat16)
    token_onehot = jnp.any(
        pair_slot.reshape(positions, TOP)[:, :, None] == slot_index[None, None, :], axis=1
    ).astype(jnp.bfloat16)
    outgoing = lax.dot_general(
        token_onehot, routed, (((0,), (0,)), ((), ())), preferred_element_type=jnp.float32
    )
    outgoing = outgoing.astype(jnp.bfloat16).reshape(experts, capacity, model_width)
    received = lax.all_to_all(outgoing, ("clip", "tm"), split_axis=0, concat_axis=0, tiled=True)
    flat_rows = received.reshape(-1, model_width)
    gate_part = jnp.dot(flat_rows, expert_gate[0], preferred_element_type=jnp.float32)
    up_part = jnp.dot(flat_rows, expert_up[0], preferred_element_type=jnp.float32)
    hidden = (jax.nn.silu(gate_part) * up_part).astype(jnp.bfloat16)
    answer = jnp.dot(hidden, expert_down[0], preferred_element_type=jnp.float32).astype(
        jnp.bfloat16
    )
    answers = lax.all_to_all(
        answer.reshape(received.shape), ("clip", "tm"), split_axis=0, concat_axis=0, tiled=True
    )
    pair_answers = jnp.dot(
        pair_onehot, answers.reshape(slot_count, model_width), preferred_element_type=jnp.float32
    )
    weighted = pair_answers.reshape(positions, TOP, model_width) * gate_values.reshape(
        positions, TOP, 1
    )
    expert_mix = jnp.sum(weighted, axis=1)
    layer_out = (second.astype(jnp.float32) + expert_mix).astype(jnp.bfloat16)
    return layer_out.reshape(tokens.shape)


def solution(mesh):
    placed = (
        P("clip", "tm", None, None),
        P("clip", "tm", None, None),
        P("clip", "tm", None, None),
        P("clip", "tm", None, None),
        P("tm", None),
        P("tm", None),
        P("tm", None),
        P("clip", None, None),
        P("clip", "tm", None, None),
        P("clip", "tm", None, None),
        P(("clip", "tm"), None, None),
        P(("clip", "tm"), None, None),
        P(("clip", "tm"), None, None),
    )
    return jax.shard_map(
        shards, mesh=mesh, in_specs=placed, out_specs=P("clip", "tm", None, None), check_vma=False
    )
```

profile of v0, /device:TPU:8, one launch (start us, length us, event | category | flops | bytes accessed | tf_op | source)
XLA Modules:
  0.0 429.1 jit_solution(4802736948756652451)
XLA Ops:
  6.5 0.7 all-gather.4.cloned.1.call-update
  7.3 0.7 all-gather.6.cloned.1.call-update
  8.1 0.7 all-gather.8.cloned.1.call-update
  8.7 1.1 copy.56
  9.9 1.1 copy.57
  11.2 2.1 fusion.71
  13.4 2.0 convolution_convert_fusion.4
  15.4 31.6 %all-gather.4.cloned.1.call-done = bf16[1024,2048]{1,0:T(8,128)(2,1)} async-done(((bf16[128,2048]{1,0:T(8,128)(2,1)}), bf16[1024,2048]{1,0:T(8,128)(2,1)}) %all-gather.4.cloned.1.call-update) | async-done | bytes 4194320 | tf_op jit(solution)/shard_map/all_gather | solution.py:113
  47.0 3.6 fusion.19
  50.6 1.2 fusion.20
  51.9 3.6 all-to-all-start
  55.5 25.5 %all-to-all-done = bf16[8,32,2048]{2,1,0:T(8,128)(2,1)S(1)} async-done(((bf16[8,32,2048]{2,1,0:T(8,128)(2,1)}), bf16[8,32,2048]{2,1,0:T(8,128)(2,1)S(1)}, u32[]{:S(2)}, u32[]{:S(2)}) %all-to-all-start) | async-done | bytes 1048608 | tf_op jit(solution)/shard_map/all_to_all | solution.py:118
  81.0 49.2 %all-gather.6.cloned.1.call-done = bf16[2048,3072]{1,0:T(8,128)(2,1)} async-done(((bf16[256,3072]{1,0:T(8,128)(2,1)}), bf16[2048,3072]{1,0:T(8,128)(2,1)}) %all-gather.6.cloned.1.call-update) | async-done | bytes 12582928 | tf_op jit(solution)/shard_map/all_gather | solution.py:70
  130.2 8.0 %convolution_convert_fusion = bf16[256,3072]{1,0:T(8,128)(2,1)S(1)} fusion(bf16[256,2048]{1,0:T(8,128)(2,1)S(1)} %bitcast.117, bf16[2048,3072]{1,0:T(8,128)(2,1)} %all-gather.6.cloned.1.call-done), kind=kOutput, calls=%fused_computation.10 | convolution fusion | flops 3222011904 | bytes 15204352 | tf_op jit(solution)/shard_map/dot_general | solution.py:30
  138.7 2.1 fusion.76
  140.8 1.8 fusion.32
  142.7 26.0 %all-gather.8.cloned.1.call-done = bf16[1024,2048]{1,0:T(8,128)(2,1)} async-done(((bf16[128,2048]{1,0:T(8,128)(2,1)}), bf16[1024,2048]{1,0:T(8,128)(2,1)}) %all-gather.8.cloned.1.call-update) | async-done | bytes 4194320 | tf_op jit(solution)/shard_map/all_gather | solution.py:81
  168.7 4.4 %convolution_convert_fusion.2 = bf16[256,2048]{1,0:T(8,128)(2,1)} fusion(bf16[1024,2048]{1,0:T(8,128)(2,1)} %all-gather.8.cloned.1.call-done, bf16[32,8,8,128]{3,2,1,0:T(8,128)(2,1)S(1)} %bitcast.124), kind=kOutput, calls=%fused_computation.22 | convolution fusion | flops 1074266112 | bytes 5767168 | tf_op jit(solution)/shard_map/dot_general | solution.py:30
  173.2 3.7 all-to-all-start.1
  177.4 1.2 reduce-window.6
  178.5 0.2 slice_reduce_fusion
  179.2 0.3 fusion.27
  179.4 12.6 %all-to-all-done.1 = bf16[8,32,2048]{2,1,0:T(8,128)(2,1)S(1)} async-done(((bf16[8,32,2048]{2,1,0:T(8,128)(2,1)}), bf16[8,32,2048]{2,1,0:T(8,128)(2,1)S(1)}, u32[]{:S(2)}, u32[]{:S(2)}) %all-to-all-start.1) | async-done | bytes 1048608 | tf_op jit(solution)/shard_map/all_to_all | solution.py:138
  192.0 0.5 fusion.22
  192.6 1.4 convolution_convert_fusion.1
  194.0 96.5 %all_to_all.20 = bf16[32,32,2048]{2,1,0:T(8,128)(2,1)S(1)} all-to-all(bf16[32,32,2048]{2,1,0:T(8,128)(2,1)S(1)} %bitcast.108), channel_id=1, replica_groups=mesh['clip'=4,'tm'=8] {'clip','tm'}, dimensions={0} | all-to-all | bytes 8388608 | tf_op jit(solution)/shard_map/all_to_all | solution.py:164
  290.5 2.0 copy-done
  292.5 8.4 %fusion.6 = f32[1024,1408]{1,0:T(8,128)} fusion(bf16[1024,2048]{1,0:T(8,128)(2,1)S(1)} %bitcast.109, bf16[1,2048,1408]{2,1,0:T(8,128)(2,1)S(1)} %bitcast.128), kind=kOutput, calls=%fused_computation.6 | convolution fusion | flops 5905580032 | bytes 15728640 | tf_op jit(solution)/shard_map/dot_general | solution.py:166
  301.0 20.6 %fusion.12 = bf16[1024,2048]{1,0:T(8,128)(2,1)} fusion(bf16[1,1408,2048]{2,1,0:T(8,128)(2,1)} %param.25, f32[1024,1408]{1,0:T(8,128)} %fusion.6, bf16[1024,2048]{1,0:T(8,128)(2,1)} %bitcast.110, bf16[1,2048,1408]{2,1,0:T(8,128)(2,1)} %param.24), kind=kOutput, calls=%fused_computation.12 | convolution fusion | flops 11821907968 | bytes 25690112 | tf_op jit(solution)/shard_map/dot_general | solution.py:169
  321.6 97.3 %all_to_all.21 = bf16[32,32,2048]{2,1,0:T(8,128)(2,1)S(1)} all-to-all(bf16[32,32,2048]{2,1,0:T(8,128)(2,1)} %bitcast.111), channel_id=1, replica_groups=mesh['clip'=4,'tm'=8] {'clip','tm'}, dimensions={0} | all-to-all | bytes 8388608 | tf_op jit(solution)/shard_map/all_to_all | solution.py:172
  418.9 2.4 multiply_reduce_fusion
  421.3 1.3 fusion.33
  (39 shorter events, 1.8 us)
Async XLA Ops:
  6.5 4.5 %copy-start.1 = (bf16[1,1,256,1024]{3,2,1,0:T(8,128)(2,1)S(1)}, bf16[1,1,256,1024]{3,2,1,0:T(8,128)(2,1)}, u32[]{:S(2)}) copy-start(bf16[1,1,256,1024]{3,2,1,0:T(8,128)(2,1)} %param.16) | copy-start | bytes 1572868
  6.5 40.5 %all-gather.4.cloned.1.call-start = ((), (), s32[]{:S(2)}) async-start(), calls=%async_computation.4 | async-start | bytes 4718592 | tf_op jit(solution)/shard_map/all_gather | solution.py:113
  7.3 123.0 %all-gather.6.cloned.1.call-start = ((), (), s32[]{:S(2)}) async-start(), calls=%async_computation.5 | async-start | bytes 14155776 | tf_op jit(solution)/shard_map/all_gather | solution.py:70
  8.0 160.7 %all-gather.8.cloned.1.call-start = ((), (), s32[]{:S(2)}) async-start(), calls=%async_computation.6 | async-start | bytes 4718592 | tf_op jit(solution)/shard_map/all_gather | solution.py:81
  13.4 33.6 %copy-start.4 = (bf16[1,1,256,2048]{3,2,1,0:T(8,128)(2,1)S(1)}, bf16[1,1,256,2048]{3,2,1,0:T(8,128)(2,1)}, u32[]{:S(2)}) copy-start(bf16[1,1,256,2048]{3,2,1,0:T(8,128)(2,1)} %param.13) | copy-start | bytes 3145732
  47.0 8.4 %copy-start.2 = (s32[1,8,8]{2,1,0:T(8,128)S(1)}, s32[1,8,8]{2,1,0:T(8,128)}, u32[]{:S(2)}) copy-start(s32[1,8,8]{2,1,0:T(8,128)} %param.20) | copy-start | bytes 772
  51.9 29.2 %all-to-all-start = ((bf16[8,32,2048]{2,1,0:T(8,128)(2,1)}), bf16[8,32,2048]{2,1,0:T(8,128)(2,1)S(1)}, u32[]{:S(2)}, u32[]{:S(2)}) async-start(bf16[8,32,2048]{2,1,0:T(8,128)(2,1)} %bitcast.4), calls=%async_computation | async-start | bytes 2097152 | tf_op jit(solution)/shard_map/all_to_all | solution.py:118
  168.7 8.2 %copy-start.3 = (s32[1,1,256,2]{2,3,1,0:T(2,128)S(1)}, s32[1,1,256,2]{2,3,1,0:T(2,128)}, u32[]{:S(2)}) copy-start(s32[1,1,256,2]{2,3,1,0:T(2,128)} %param.21) | copy-start | bytes 6148
  173.2 18.9 %all-to-all-start.1 = ((bf16[8,32,2048]{2,1,0:T(8,128)(2,1)}), bf16[8,32,2048]{2,1,0:T(8,128)(2,1)S(1)}, u32[]{:S(2)}, u32[]{:S(2)}) async-start(bf16[8,32,2048]{2,1,0:T(8,128)(2,1)} %bitcast.9), calls=%async_computation.1 | async-start | bytes 2097152 | tf_op jit(solution)/shard_map/all_to_all | solution.py:138
  192.0 100.5 %slice-start = ((s8[5767168]{0:T(1024)(128)(4,1)}), s8[4194304]{0:T(1024)(128)(4,1)S(1)}, s32[]{:S(2)}) async-start(s8[5767168]{0:T(1024)(128)(4,1)} %bitcast.127), calls=%async_computation.7 | async-start | bytes 8388608
  192.6 99.9 %slice-start.1 = ((s8[5767168]{0:T(1024)(128)(4,1)}), s8[1572864]{0:T(1024)(128)(4,1)S(1)}, s32[]{:S(2)}) async-start(s8[5767168]{0:T(1024)(128)(4,1)} %bitcast.127), calls=%async_computation.8 | async-start | bytes 3145728
  290.5 2.0 copy-start
  321.6 97.3 %copy-start.5 = (f32[1,1,256,2]{2,3,1,0:T(2,128)S(1)}, f32[1,1,256,2]{2,3,1,0:T(2,128)}, u32[]{:S(2)}) copy-start(f32[1,1,256,2]{2,3,1,0:T(2,128)} %param.22) | copy-start | bytes 6148
Sparse Core Ops, SparseCore 0:
  9.2 37.7 all-gather.3
  48.9 81.2 all-gather.5
  132.1 36.5 all-gather.7
where the time goes:
time: 432 us; the launch traced here: 429 us
  blocking collectives  194 us (45%)
  waiting for transfers between devices  147 us (34%)
  matrix products  57 us (13%)
  between operations  13.3 us (3%)
  starting transfers between devices  7.38 us (2%)
  local copies, waits for them, and re-layouts  5.99 us (1%)
  other arithmetic  4.69 us (1%)
    all_to_all x1, blocking collectives, shards(): lax.all_to_all(answer.reshape(received.shape), ('clip', 'tm'), split_axis...  97.3 us
    all_to_all x1, blocking collectives, shards(): lax.all_to_all(outgoing, ('clip', 'tm'), split_axis=0, concat_axis=0, til...  96.5 us
    all_gather x1, waiting for transfers between devices, temporal_inputs(): lax.all_gather(qkv_rows, 'tm', axis=0, tiled=True)  49.2 us
    all_gather x1, waiting for transfers between devices, shards(): lax.all_gather(spatial_proj, 'tm', axis=0, tiled=True)  31.6 us
    all_gather x1, waiting for transfers between devices, temporal_output(): lax.all_gather(proj_rows, 'tm', axis=0, tiled=True)  26 us
    all_to_all x1, waiting for transfers between devices, shards(): lax.all_to_all(normed.reshape(tm_count, per_block, model_width), 'tm', sp...  25.5 us
    dot_general x1, matrix products, shards(): jnp.dot(hidden, expert_down[0], preferred_element_type=jnp.float32)  20.6 us
    dot_general x3, matrix products, add_columns(): return jnp.dot(left_side, piece, preferred_element_type=jnp.float32)  16.1 us
  transfers between devices with their start and end apart: 5, of which 5 were waited for; matrix products, arithmetic and copies ran while one was open for 6% of the time, Pallas kernels for 0%

commit v1 on v0

--- a/solution.py
+++ b/solution.py
@@ -1,8 +1,11 @@
+import functools
 import math
 
 import jax
 import jax.numpy as jnp
 from jax import lax
+from jax.experimental import pallas as pl
+from jax.experimental.pallas import tpu as pltpu
 from jax.sharding import PartitionSpec as P
 
 HEADS = 8
@@ -80,6 +83,318 @@
     return fold_rows(
         zero_start, lax.all_gather(proj_rows, "tm", axis=0, tiled=True), jnp.int32(0)
     ).astype(jnp.bfloat16)
+
+
+LINK = pl.DeviceIdType.MESH
+VMEM_BYTES = 60 * 1024 * 1024
+
+
+def column_chunks(width):
+    return 4 if width % 512 == 0 else 1
+
+
+def greet(neighbours_line, plane_count):
+    z = lax.axis_index("clip")
+    me = lax.axis_index("tm")
+    barrier = pltpu.get_barrier_semaphore()
+    for step in range(1, plane_count):
+        pl.semaphore_signal(
+            barrier,
+            inc=1,
+            device_id={"tm": lax.rem(me + step, plane_count)},
+            device_id_type=LINK,
+        )
+
+    @pl.when(z > 0)
+    def _():
+        pl.semaphore_signal(barrier, inc=1, device_id={"clip": z - 1}, device_id_type=LINK)
+
+    @pl.when(z < neighbours_line - 1)
+    def _():
+        pl.semaphore_signal(barrier, inc=1, device_id={"clip": z + 1}, device_id_type=LINK)
+
+    ends = (z == 0) | (z == neighbours_line - 1)
+
+    @pl.when(ends)
+    def _():
+        pl.semaphore_wait(barrier, plane_count)
+
+    @pl.when(jnp.logical_not(ends))
+    def _():
+        pl.semaphore_wait(barrier, plane_count + 1)
+
+
+def dispatch_kernel(
+    n, m, chunks, x_ref, pick_ref, out_ref, frames, stage, zsend, zrecv, xsend, xrecv, own_sem, loc
+):
+    z = lax.axis_index("clip")
+    me = lax.axis_index("tm")
+    width = x_ref.shape[1]
+    cap = stage.shape[2]
+    w = width // chunks
+    first_copy = pltpu.make_async_copy(x_ref, frames.at[z], own_sem)
+    first_copy.start()
+    greet(n, m)
+    first_copy.wait()
+
+    def columns(c):
+        return pl.ds(pl.multiple_of(c * w, w), w)
+
+    def line_copy(to, f, s, c, way):
+        return pltpu.make_async_remote_copy(
+            src_ref=frames.at[f, :, columns(c)],
+            dst_ref=frames.at[f, :, columns(c)],
+            send_sem=zsend.at[way, s, c],
+            recv_sem=zrecv.at[f, c],
+            device_id={"clip": to},
+            device_id_type=LINK,
+        )
+
+    def spread(f, c):
+        rows = jnp.dot(
+            pick_ref[f], frames[f, :, columns(c)], preferred_element_type=jnp.float32
+        )
+        for t in range(m):
+            stage[f, t, :, columns(c)] = rows[t * cap : (t + 1) * cap].astype(jnp.bfloat16)
+        for t in range(1, m):
+            to = lax.rem(me + t, m)
+            pltpu.make_async_remote_copy(
+                src_ref=stage.at[f, to, :, columns(c)],
+                dst_ref=out_ref.at[me, f, :, columns(c)],
+                send_sem=xsend.at[t],
+                recv_sem=xrecv.at[t],
+                device_id={"tm": to},
+                device_id_type=LINK,
+            ).start()
+        pltpu.make_async_copy(
+            stage.at[f, me, :, columns(c)], out_ref.at[me, f, :, columns(c)], loc
+        ).start()
+
+    def step(i, carry):
+        s = i // chunks
+        c = lax.rem(i, chunks)
+        for way in (0, 1):
+            f = z - s if way == 0 else z + s
+            to = z + 1 if way == 0 else z - 1
+            here = f >= 0 if way == 0 else f <= n - 1
+            onward = z < n - 1 if way == 0 else z > 0
+
+            @pl.when(here & (s > 0))
+            def _(f=f, c=c, s=s, to=to, way=way):
+                line_copy(to, f, s, c, way).wait_recv()
+
+            @pl.when(here & onward)
+            def _(f=f, c=c, s=s, to=to, way=way):
+                line_copy(to, f, s, c, way).start()
+
+        for way in (0, 1):
+            f = z - s if way == 0 else z + s
+            here = f >= 0 if way == 0 else (f <= n - 1) & (s > 0)
+
+            @pl.when(here)
+            def _(f=f, c=c):
+                spread(f, c)
+
+        return carry
+
+    lax.fori_loop(0, n * chunks, step, 0)
+
+    def finish(i, carry):
+        s = i // chunks
+        c = lax.rem(i, chunks)
+        for way in (0, 1):
+            f = z - s if way == 0 else z + s
+            to = z + 1 if way == 0 else z - 1
+            here = f >= 0 if way == 0 else f <= n - 1
+            onward = z < n - 1 if way == 0 else z > 0
+
+            @pl.when(here & onward)
+            def _(f=f, c=c, s=s, to=to, way=way):
+                line_copy(to, f, s, c, way).wait_send()
+
+        return carry
+
+    lax.fori_loop(0, n * chunks, finish, 0)
+    for t in range(1, m):
+        to = lax.rem(me + t, m)
+        whole = pltpu.make_async_remote_copy(
+            src_ref=stage.at[:, to],
+            dst_ref=out_ref.at[lax.rem(me + m - t, m)],
+            send_sem=xsend.at[t],
+            recv_sem=xrecv.at[t],
+            device_id={"tm": to},
+            device_id_type=LINK,
+        )
+        whole.wait_send()
+        whole.wait_recv()
+    pltpu.make_async_copy(stage.at[:, me], out_ref.at[me], loc).wait()
+
+
+def dispatch(routed, pick, cap):
+    n, m = lax.axis_size("clip"), lax.axis_size("tm")
+    rows, width = routed.shape
+    chunks = column_chunks(width)
+    return pl.pallas_call(
+        functools.partial(dispatch_kernel, n, m, chunks),
+        out_shape=jax.ShapeDtypeStruct((m, n, cap, width), jnp.bfloat16),
+        in_specs=[pl.BlockSpec(memory_space=pl.ANY), pl.BlockSpec(memory_space=pltpu.VMEM)],
+        out_specs=pl.BlockSpec(memory_space=pltpu.VMEM),
+        scratch_shapes=[
+            pltpu.VMEM((n, rows, width), jnp.bfloat16),
+            pltpu.VMEM((n, m, cap, width), jnp.bfloat16),
+            pltpu.SemaphoreType.DMA((2, n, chunks)),
+            pltpu.SemaphoreType.DMA((n, chunks)),
+            pltpu.SemaphoreType.DMA((m,)),
+            pltpu.SemaphoreType.DMA((m,)),
+            pltpu.SemaphoreType.DMA,
+            pltpu.SemaphoreType.DMA,
+        ],
+        compiler_params=pltpu.CompilerParams(
+            collective_id=1, has_side_effects=True, vmem_limit_bytes=VMEM_BYTES
+        ),
+    )(routed, pick)
+
+
+def combine_kernel(
+    n, m, chunks, ans_ref, mix_ref, base_ref, out_ref, got, zin, zout, total, zsend, zrecv, xsend, xrecv
+):
+    z = lax.axis_index("clip")
+    me = lax.axis_index("tm")
+    width = base_ref.shape[1]
+    cap = got.shape[2]
+    w = width // chunks
+    greet(n, m)
+
+    def columns(c):
+        return pl.ds(pl.multiple_of(c * w, w), w)
+
+    def send_plane(f, c):
+        for t in range(1, m):
+            to = lax.rem(me + t, m)
+            pltpu.make_async_remote_copy(
+                src_ref=ans_ref.at[to, f, :, columns(c)],
+                dst_ref=got.at[me, f, :, columns(c)],
+                send_sem=xsend.at[t],
+                recv_sem=xrecv.at[f, c],
+                device_id={"tm": to},
+                device_id_type=LINK,
+            ).start()
+        pltpu.make_async_copy(
+            ans_ref.at[me, f, :, columns(c)], got.at[me, f, :, columns(c)], xrecv.at[f, c]
+        ).start()
+
+    def ordered(act):
+        def step(i, carry):
+            s = i // chunks
+            c = lax.rem(i, chunks)
+            for way in (0, 1):
+                f = n - 1 - s if way == 0 else s
+
+                @pl.when(f > z if way == 0 else f < z)
+                def _(f=f, c=c, way=way):
+                    act(f, c, way)
+
+            return carry
+
+        lax.fori_loop(0, n * chunks, step, 0)
+
+        def last(c, carry):
+            act(z, c, 2)
+            return carry
+
+        lax.fori_loop(0, chunks, last, 0)
+
+    ordered(lambda f, c, way: send_plane(f, c))
+
+    def line_copy(f, c, way):
+        return pltpu.make_async_remote_copy(
+            src_ref=zout.at[f, :, columns(c)],
+            dst_ref=zin.at[f + 1 - way, :, columns(c)],
+            send_sem=zsend.at[f, c],
+            recv_sem=zrecv.at[f + 1 - way, c],
+            device_id={"clip": z + 1 - 2 * way},
+            device_id_type=LINK,
+        )
+
+    def add_line(f, c, way):
+        line_copy(f, c, way).wait_recv()
+        total[...] += zin[f + 1 - way, :, columns(c)].astype(jnp.float32)
+
+    def work(f, c, way):
+        pltpu.make_async_copy(
+            got.at[:, f, :, columns(c)], got.at[:, f, :, columns(c)], xrecv.at[f, c]
+        ).wait()
+        if cap % 16 == 0:
+            slots = got[:, f, :, columns(c)].reshape(m * cap, w)
+        else:
+            slots = jnp.concatenate(
+                [got[t, f, :, columns(c)].astype(jnp.float32) for t in range(m)], axis=0
+            ).astype(jnp.bfloat16)
+        total[...] = jnp.dot(mix_ref[f], slots, preferred_element_type=jnp.float32)
+        if way != 1:
+
+            @pl.when(z > 0)
+            def _():
+                add_line(f, c, 0)
+
+        if way != 0:
+
+            @pl.when(z < n - 1)
+            def _():
+                add_line(f, c, 1)
+
+        if way == 2:
+            out_ref[:, columns(c)] = (
+                base_ref[:, columns(c)].astype(jnp.float32) + total[...]
+            ).astype(jnp.bfloat16)
+        else:
+            zout[f, :, columns(c)] = total[...].astype(jnp.bfloat16)
+            line_copy(f, c, way).start()
+
+    ordered(work)
+
+    def finish(f, c, way):
+        if way != 2:
+            line_copy(f, c, way).wait_send()
+
+    ordered(finish)
+    for t in range(1, m):
+        to = lax.rem(me + t, m)
+        pltpu.make_async_remote_copy(
+            src_ref=ans_ref.at[to],
+            dst_ref=got.at[me],
+            send_sem=xsend.at[t],
+            recv_sem=xrecv.at[0, 0],
+            device_id={"tm": to},
+            device_id_type=LINK,
+        ).wait_send()
+
+
+def combine(answers, mix, base):
+    n, m = lax.axis_size("clip"), lax.axis_size("tm")
+    rows, width = base.shape
+    cap = answers.shape[2]
+    chunks = column_chunks(width)
+    vmem = pl.BlockSpec(memory_space=pltpu.VMEM)
+    return pl.pallas_call(
+        functools.partial(combine_kernel, n, m, chunks),
+        out_shape=jax.ShapeDtypeStruct((rows, width), jnp.bfloat16),
+        in_specs=[pl.BlockSpec(memory_space=pl.ANY), vmem, vmem],
+        out_specs=vmem,
+        scratch_shapes=[
+            pltpu.VMEM((m, n, cap, width), jnp.bfloat16),
+            pltpu.VMEM((n + 1, rows, width), jnp.bfloat16),
+            pltpu.VMEM((n, rows, width), jnp.bfloat16),
+            pltpu.VMEM((rows, width // chunks), jnp.float32),
+            pltpu.SemaphoreType.DMA((n, chunks)),
+            pltpu.SemaphoreType.DMA((n + 1, chunks)),
+            pltpu.SemaphoreType.DMA((m,)),
+            pltpu.SemaphoreType.DMA((n, chunks)),
+        ],
+        compiler_params=pltpu.CompilerParams(
+            collective_id=2, has_side_effects=True, vmem_limit_bytes=VMEM_BYTES
+        ),
+    )(answers, mix, base)
 
 
 def shards(
@@ -146,22 +461,26 @@
     second = (first.astype(jnp.float32) + temporal_update.astype(jnp.float32)).astype(jnp.bfloat16)
     routed = rms_normed(second)
     capacity = 2 * TOP * positions // experts
-    slot_count = experts * capacity
     pair_ids = expert_ids.reshape(positions * TOP)
     chosen = (pair_ids[:, None] == jnp.arange(experts, dtype=jnp.int32)[None, :]).astype(jnp.int32)
     earlier = jnp.cumsum(chosen, axis=0) - chosen
     pair_rank = jnp.sum(earlier * chosen, axis=1)
     pair_slot = pair_ids * capacity + pair_rank
-    slot_index = jnp.arange(slot_count, dtype=jnp.int32)
-    pair_onehot = (pair_slot[:, None] == slot_index[None, :]).astype(jnp.bfloat16)
-    token_onehot = jnp.any(
-        pair_slot.reshape(positions, TOP)[:, :, None] == slot_index[None, None, :], axis=1
-    ).astype(jnp.bfloat16)
-    outgoing = lax.dot_general(
-        token_onehot, routed, (((0,), (0,)), ((), ())), preferred_element_type=jnp.float32
-    )
-    outgoing = outgoing.astype(jnp.bfloat16).reshape(experts, capacity, model_width)
-    received = lax.all_to_all(outgoing, ("clip", "tm"), split_axis=0, concat_axis=0, tiled=True)
+    told = jnp.stack([pair_slot.astype(jnp.float32), gate_values.reshape(positions * TOP)])
+    told = lax.all_gather(told, "clip", axis=0)
+    plane_slots = tm_count * capacity
+    slots_here = told[:, 0].astype(jnp.int32) - lax.axis_index("clip") * plane_slots
+    slots_here = slots_here.reshape(clip_count, positions, TOP)
+    gates_here = told[:, 1].reshape(clip_count, positions, TOP)
+    slot_index = jnp.arange(plane_slots, dtype=jnp.int32)
+    pick = jnp.zeros((clip_count, plane_slots, positions), jnp.bool_)
+    mix = jnp.zeros((clip_count, positions, plane_slots), jnp.float32)
+    for k in range(TOP):
+        pick = pick | (slots_here[:, None, :, k] == slot_index[None, :, None])
+        mix = mix + jnp.where(
+            slots_here[:, :, k, None] == slot_index[None, None, :], gates_here[:, :, k, None], 0.0
+        )
+    received = dispatch(routed, pick.astype(jnp.bfloat16), capacity)
     flat_rows = received.reshape(-1, model_width)
     gate_part = jnp.dot(flat_rows, expert_gate[0], preferred_element_type=jnp.float32)
     up_part = jnp.dot(flat_rows, expert_up[0], preferred_element_type=jnp.float32)
@@ -169,17 +488,7 @@
     answer = jnp.dot(hidden, expert_down[0], preferred_element_type=jnp.float32).astype(
         jnp.bfloat16
     )
-    answers = lax.all_to_all(
-        answer.reshape(received.shape), ("clip", "tm"), split_axis=0, concat_axis=0, tiled=True
-    )
-    pair_answers = jnp.dot(
-        pair_onehot, answers.reshape(slot_count, model_width), preferred_element_type=jnp.float32
-    )
-    weighted = pair_answers.reshape(positions, TOP, model_width) * gate_values.reshape(
-        positions, TOP, 1
-    )
-    expert_mix = jnp.sum(weighted, axis=1)
-    layer_out = (second.astype(jnp.float32) + expert_mix).astype(jnp.bfloat16)
+    layer_out = combine(answer.reshape(received.shape), mix.astype(jnp.bfloat16), second)
     return layer_out.reshape(tokens.shape)
 
 

time: 432 us -> 411 us (0.951)
  blocking collectives: 194 us -> 13.3 us
  Pallas kernels: 0 us -> 176 us
  waiting for transfers between devices: 147 us -> 130 us
    all_to_all x2 -> x0, blocking collectives: 194 us -> none  [the longest x1 97.3 us: shards(): lax.all_to_all(answer.reshape(received.shape), ('clip', 'tm'), split_axis...]
    pallas_call x0 -> x2, Pallas kernels: none -> 176 us  [the longest x1 103 us: combine(): pl.pallas_call(functools.partial(combine_kernel, n, m, chunks), out_shape...]
    all_to_all x1, waiting for transfers between devices: 25.5 us -> 10.9 us  [shards(): lax.all_to_all(normed.reshape(tm_count, per_block, model_width), 'tm', sp...]
    all_gather x0 -> x1, blocking collectives: none -> 13.3 us  [shards(): told = lax.all_gather(told, 'clip', axis=0)]
  transfers between devices with their start and end apart: 5 -> 5, of which waited for: 5 -> 5; matrix products, arithmetic and copies ran while one was open for 6% -> 7% of each run, Pallas kernels for 0% -> 0%
where the time goes in v1:
time: 411 us
  Pallas kernels  176 us (43%)
  waiting for transfers between devices  130 us (32%)
  matrix products  56.5 us (14%)
  between operations  13.4 us (3%)
  blocking collectives  13.3 us (3%)
  local copies, waits for them, and re-layouts  7.65 us (2%)
  starting transfers between devices  7.38 us (2%)
  other arithmetic  6.87 us (2%)
    pallas_call x1, Pallas kernels, combine(): pl.pallas_call(functools.partial(combine_kernel, n, m, chunks), out_shape...  103 us
    pallas_call x1, Pallas kernels, dispatch(): pl.pallas_call(functools.partial(dispatch_kernel, n, m, chunks), out_shap...  72.2 us
    all_gather x1, waiting for transfers between devices, temporal_inputs(): lax.all_gather(qkv_rows, 'tm', axis=0, tiled=True)  49.2 us
    all_gather x1, waiting for transfers between devices, shards(): lax.all_gather(spatial_proj, 'tm', axis=0, tiled=True)  30.1 us
    all_gather x1, waiting for transfers between devices, temporal_output(): lax.all_gather(proj_rows, 'tm', axis=0, tiled=True)  26 us
    dot_general x1, matrix products, shards(): jnp.dot(hidden, expert_down[0], preferred_element_type=jnp.float32)  20.6 us
    dot_general x3, matrix products, add_columns(): return jnp.dot(left_side, piece, preferred_element_type=jnp.float32)  16 us
    all_gather x1, blocking collectives, shards(): told = lax.all_gather(told, 'clip', axis=0)  13.3 us
  transfers between devices with their start and end apart: 5, of which 5 were waited for; matrix products, arithmetic and copies ran while one was open for 7% of the time, Pallas kernels for 0%

profile of v1, /device:TPU:8, one launch (start us, length us, event | category | flops | bytes accessed | tf_op | source)
XLA Modules:
  0.0 410.6 jit_solution(5062731469342415532)
XLA Ops:
  6.5 0.7 all-gather.6.cloned.1.call-update
  7.3 0.7 all-gather.8.cloned.1.call-update
  8.1 0.7 all-gather.10.cloned.1.call-update
  8.7 1.1 copy.95
  9.9 1.1 copy.96
  11.6 1.2 reduce-window.6
  12.8 2.1 fusion.69
  14.9 2.0 convolution_convert_fusion.3
  16.9 30.1 %all-gather.6.cloned.1.call-done = bf16[1024,2048]{1,0:T(8,128)(2,1)} async-done(((bf16[128,2048]{1,0:T(8,128)(2,1)}), bf16[1024,2048]{1,0:T(8,128)(2,1)}) %all-gather.6.cloned.1.call-update) | async-done | bytes 4194320 | tf_op jit(solution)/shard_map/all_gather | solution.py:428
  47.0 3.6 fusion.21
  50.6 1.2 fusion.22
  51.9 3.6 all-to-all-start
  55.4 0.2 slice_reduce_fusion
  56.6 13.3 %all-gather.1 = f32[4,2,512]{2,1,0:T(2,128)S(1)} all-gather(f32[1,2,512]{2,1,0:T(2,128)S(1)} %maximum_bitcast_fusion), channel_id=2, replica_groups=mesh['clip'=4,'tm'=8] {'clip'}, dimensions={0}, use_global_device_ids=true | all-gather | bytes 20480 | tf_op jit(solution)/shard_map/all_gather | solution.py:470
  70.1 10.9 %all-to-all-done = bf16[8,32,2048]{2,1,0:T(8,128)(2,1)S(1)} async-done(((bf16[8,32,2048]{2,1,0:T(8,128)(2,1)}), bf16[8,32,2048]{2,1,0:T(8,128)(2,1)S(1)}, u32[]{:S(2)}, u32[]{:S(2)}) %all-to-all-start) | async-done | bytes 1048608 | tf_op jit(solution)/shard_map/all_to_all | solution.py:433
  81.0 49.2 %all-gather.8.cloned.1.call-done = bf16[2048,3072]{1,0:T(8,128)(2,1)} async-done(((bf16[256,3072]{1,0:T(8,128)(2,1)}), bf16[2048,3072]{1,0:T(8,128)(2,1)}) %all-gather.8.cloned.1.call-update) | async-done | bytes 12582928 | tf_op jit(solution)/shard_map/all_gather | solution.py:73
  130.2 8.0 %convolution_convert_fusion = bf16[256,3072]{1,0:T(8,128)(2,1)S(1)} fusion(bf16[256,2048]{1,0:T(8,128)(2,1)S(1)} %bitcast.116, bf16[2048,3072]{1,0:T(8,128)(2,1)} %all-gather.8.cloned.1.call-done), kind=kOutput, calls=%fused_computation.9 | convolution fusion | flops 3222011904 | bytes 15204352 | tf_op jit(solution)/shard_map/dot_general | solution.py:33
  138.7 2.1 fusion.74
  140.8 1.8 fusion.28
  142.7 26.0 %all-gather.10.cloned.1.call-done = bf16[1024,2048]{1,0:T(8,128)(2,1)} async-done(((bf16[128,2048]{1,0:T(8,128)(2,1)}), bf16[1024,2048]{1,0:T(8,128)(2,1)}) %all-gather.10.cloned.1.call-update) | async-done | bytes 4194320 | tf_op jit(solution)/shard_map/all_gather | solution.py:84
  168.7 4.4 %convolution_convert_fusion.1 = bf16[256,2048]{1,0:T(8,128)(2,1)} fusion(bf16[1024,2048]{1,0:T(8,128)(2,1)} %all-gather.10.cloned.1.call-done, bf16[32,8,8,128]{3,2,1,0:T(8,128)(2,1)S(1)} %bitcast.127), kind=kOutput, calls=%fused_computation.19 | convolution fusion | flops 1074266112 | bytes 5767168 | tf_op jit(solution)/shard_map/dot_general | solution.py:33
  173.1 3.7 all-to-all-start.1
  177.8 1.1 fusion.31.pick_ref
  178.9 1.4 add_convert_fusion.mix_ref
  180.3 11.8 %all-to-all-done.1 = bf16[8,32,2048]{2,1,0:T(8,128)(2,1)S(1)} async-done(((bf16[8,32,2048]{2,1,0:T(8,128)(2,1)}), bf16[8,32,2048]{2,1,0:T(8,128)(2,1)S(1)}, u32[]{:S(2)}, u32[]{:S(2)}) %all-to-all-start.1) | async-done | bytes 1048608 | tf_op jit(solution)/shard_map/all_to_all | solution.py:453
  192.0 0.5 fusion.19
  192.6 1.3 fusion.20.x_ref
  193.9 72.2 %shard_map.127 = bf16[8,4,32,2048]{3,2,1,0:T(8,128)(2,1)} custom-call(bf16[256,2048]{1,0:T(8,128)(2,1)} %fusion.20.x_ref, bf16[4,256,256]{2,1,0:T(8,128)(2,1)} %fusion.31.pick_ref), custom_call_target="tpu_custom_call" | custom-call | tf_op jit(solution)/shard_map/pallas_call | solution.py:237
  266.1 11.7 %fusion.6 = f32[1024,1408]{1,0:T(8,128)} fusion(bf16[1024,2048]{1,0:T(8,128)(2,1)} %bitcast.108, bf16[1,2048,1408]{2,1,0:T(8,128)(2,1)} %param.23), kind=kOutput, calls=%fused_computation.6 | convolution fusion | flops 5905580032 | bytes 15728640 | tf_op jit(solution)/shard_map/dot_general | solution.py:485
  277.9 20.6 %fusion.12 = bf16[1024,2048]{1,0:T(8,128)(2,1)} fusion(bf16[1,1408,2048]{2,1,0:T(8,128)(2,1)} %param.25, f32[1024,1408]{1,0:T(8,128)} %fusion.6, bf16[1024,2048]{1,0:T(8,128)(2,1)} %bitcast.109, bf16[1,2048,1408]{2,1,0:T(8,128)(2,1)} %param.24), kind=kOutput, calls=%fused_computation.10 | convolution fusion | flops 11821907968 | bytes 25690112 | tf_op jit(solution)/shard_map/dot_general | solution.py:488
  298.5 103.3 %shard_map.128 = bf16[256,2048]{1,0:T(8,128)(2,1)} custom-call(bf16[8,4,32,2048]{3,2,1,0:T(8,128)(2,1)} %bitcast.110, bf16[4,256,256]{2,1,0:T(8,128)(2,1)} %add_convert_fusion.mix_ref, bf16[256,2048]{1,0:T(8,128)(2,1)} %copy-done), custom_call_target="tpu_custom_call" | custom-call | tf_op jit(solution)/shard_map/pallas_call | solution.py:379
  401.8 2.3 copy.144
  (49 shorter events, 3.1 us)
Async XLA Ops:
  6.5 4.5 %copy-start.1 = (bf16[1,1,256,1024]{3,2,1,0:T(8,128)(2,1)S(1)}, bf16[1,1,256,1024]{3,2,1,0:T(8,128)(2,1)}, u32[]{:S(2)}) copy-start(bf16[1,1,256,1024]{3,2,1,0:T(8,128)(2,1)} %param.16) | copy-start | bytes 1572868
  6.5 4.7 %copy-start.2 = (s32[1,1,256,2]{2,3,1,0:T(2,128)S(1)}, s32[1,1,256,2]{2,3,1,0:T(2,128)}, u32[]{:S(2)}) copy-start(s32[1,1,256,2]{2,3,1,0:T(2,128)} %param.21) | copy-start | bytes 6148
  6.5 6.2 %copy-start.3 = (s32[1,8,8]{2,1,0:T(8,128)S(1)}, s32[1,8,8]{2,1,0:T(8,128)}, u32[]{:S(2)}) copy-start(s32[1,8,8]{2,1,0:T(8,128)} %param.20) | copy-start | bytes 772
  6.5 40.5 %all-gather.6.cloned.1.call-start = ((), (), s32[]{:S(2)}) async-start(), calls=%async_computation.2 | async-start | bytes 4718592 | tf_op jit(solution)/shard_map/all_gather | solution.py:428
  7.3 122.9 %all-gather.8.cloned.1.call-start = ((), (), s32[]{:S(2)}) async-start(), calls=%async_computation.3 | async-start | bytes 14155776 | tf_op jit(solution)/shard_map/all_gather | solution.py:73
  8.0 160.7 %all-gather.10.cloned.1.call-start = ((), (), s32[]{:S(2)}) async-start(), calls=%async_computation.4 | async-start | bytes 4718592 | tf_op jit(solution)/shard_map/all_gather | solution.py:84
  14.9 32.1 %copy-start.5 = (bf16[1,1,256,2048]{3,2,1,0:T(8,128)(2,1)S(1)}, bf16[1,1,256,2048]{3,2,1,0:T(8,128)(2,1)}, u32[]{:S(2)}) copy-start(bf16[1,1,256,2048]{3,2,1,0:T(8,128)(2,1)} %param.13) | copy-start | bytes 3145732
  50.6 5.6 %copy-start.4 = (f32[1,1,256,2]{2,3,1,0:T(2,128)S(1)}, f32[1,1,256,2]{2,3,1,0:T(2,128)}, u32[]{:S(2)}) copy-start(f32[1,1,256,2]{2,3,1,0:T(2,128)} %param.22) | copy-start | bytes 6148
  51.9 29.1 %all-to-all-start = ((bf16[8,32,2048]{2,1,0:T(8,128)(2,1)}), bf16[8,32,2048]{2,1,0:T(8,128)(2,1)S(1)}, u32[]{:S(2)}, u32[]{:S(2)}) async-start(bf16[8,32,2048]{2,1,0:T(8,128)(2,1)} %bitcast.4), calls=%async_computation | async-start | bytes 2097152 | tf_op jit(solution)/shard_map/all_to_all | solution.py:433
  173.1 18.9 %all-to-all-start.1 = ((bf16[8,32,2048]{2,1,0:T(8,128)(2,1)}), bf16[8,32,2048]{2,1,0:T(8,128)(2,1)S(1)}, u32[]{:S(2)}, u32[]{:S(2)}) async-start(bf16[8,32,2048]{2,1,0:T(8,128)(2,1)} %bitcast.9), calls=%async_computation.1 | async-start | bytes 2097152 | tf_op jit(solution)/shard_map/all_to_all | solution.py:453
  192.5 85.3 %copy-start = (bf16[256,2048]{1,0:T(8,128)(2,1)}, bf16[256,2048]{1,0:T(8,128)(2,1)S(1)}, u32[]{:S(2)}) copy-start(bf16[256,2048]{1,0:T(8,128)(2,1)S(1)} %get-tuple-element.6.base_ref) | copy-start | bytes 3145732
Sparse Core Ops, SparseCore 0:
  9.2 37.7 all-gather.5
  48.9 81.2 all-gather.7
  132.1 36.5 all-gather.9
